TPU v7x, 32 devices: a whole 2x2x4 slice. The times are simulated.
32 devices in a mesh: dp: 8 (over y, x, core), mp: 4 (over z).
Axes of the slice: x: 2, y: 2, z: 4, core: 2. Of those that a mesh axis runs over, the one named last changes fastest.
Arguments:
- layer_input: bfloat16 [32, 8192], P('dp'), may hold values from -6 to 6
- pre_act: bfloat16 [32, 8192], P('dp', 'mp'), may hold values from -8 to 8
- hidden_adjoint: bfloat16 [32, 8192], P('dp', 'mp'), may hold values from -6 to 6
- output_adjoint: bfloat16 [32, 8192], P('dp', 'mp'), may hold values from -6 to 6
Outputs:
- precond_in: float32 [8192, 8192], P('dp', 'mp')
- direction_in: float32 [8192, 8192], P('dp', 'mp')
- precond_out: float32 [8192, 8192], P('dp', 'mp')
- direction_out: float32 [8192, 8192], P('dp', 'mp')
- sq_norm: float32 [], replicated
All inputs are finite; a program needn't handle non-finite values.
Results may differ from a plain program's by a relative error of at most 0.0029.
Values may be sent and summed in bfloat16 or wider, within the bound.
A program may use at most 64 MiB of HBM per device.

v0:
```python
import jax
import jax.numpy as jnp
from jax import lax
from jax.sharding import PartitionSpec as P

D = 8192
H = 8192
DAMPING = 0.1
EXPONENT = 0.75


def square_bf(values):
    wide = values.astype(jnp.float32)
    return (wide * wide).astype(jnp.bfloat16)


def accumulate(act_block, sq_block, adj_piece):
    contract = (((0,), (0,)), ((), ()))
    grad_sum = lax.dot_general(act_block, adj_piece, contract, preferred_element_type=jnp.float32)
    square_sum = lax.dot_general(
        sq_block, square_bf(adj_piece), contract, preferred_element_type=jnp.float32
    )
    return (grad_sum, square_sum)


def finish(partial_value, total_rows):
    gradient = partial_value[0] / total_rows
    precond = (partial_value[1] / total_rows + DAMPING) ** EXPONENT
    norm_term = jnp.sum(gradient * gradient / precond)
    return (gradient, precond, norm_term)


def shards(layer_input, pre_act, hidden_adjoint, output_adjoint):
    preact = pre_act.astype(jnp.float32)
    logistic = jax.nn.sigmoid(preact)
    hidden = (preact * logistic).astype(jnp.bfloat16)
    adjoint = (
        hidden_adjoint.astype(jnp.float32) * logistic * (1.0 + preact * (1.0 - logistic))
    ).astype(jnp.bfloat16)
    own_input = lax.all_to_all(layer_input, "dp", split_axis=1, concat_axis=0, tiled=True)
    sq_input = square_bf(own_input)
    total_rows = own_input.shape[0]
    wide_hidden = lax.all_gather(hidden, "mp", axis=1, tiled=True)
    own_hidden = lax.all_to_all(wide_hidden, "dp", split_axis=1, concat_axis=0, tiled=True)
    sq_hidden = square_bf(own_hidden)
    sums_in = accumulate(own_input, sq_input, lax.all_gather(adjoint, "dp", axis=0, tiled=True))
    sums_out = accumulate(
        own_hidden, sq_hidden, lax.all_gather(output_adjoint, "dp", axis=0, tiled=True)
    )
    gradient_in, precond_in, term_in = finish(sums_in, total_rows)
    gradient_out, precond_out, term_out = finish(sums_out, total_rows)
    sq_norm = lax.psum(term_in + term_out, ("dp", "mp"))
    rescale = jnp.sqrt(2.0 * D * H / sq_norm)
    direction_in = gradient_in / precond_in * rescale
    direction_out = gradient_out / precond_out * rescale
    return (precond_in, direction_in, precond_out, direction_out, sq_norm)


def solution(mesh):
    placed = (P("dp", None), P("dp", "mp"), P("dp", "mp"), P("dp", "mp"))
    return jax.shard_map(
        shards,
        mesh=mesh,
        in_specs=placed,
        out_specs=(P("dp", "mp"), P("dp", "mp"), P("dp", "mp"), P("dp", "mp"), P()),
        check_vma=False,
    )
```

profile of v0, /device:TPU:0, one launch (start us, length us, event | category | flops | bytes accessed | tf_op | source)
XLA Modules:
  0.0 133.4 jit_solution(15350232104087235126)
XLA Ops:
  0.6 5.2 %all-to-all-start = ((bf16[4,8,1024]{2,0,1:T(4,128)(2,1)}), bf16[4,8,1024]{2,0,1:T(4,128)(2,1)S(1)}, u32[]{:S(2)}, u32[]{:S(2)}) async-start(bf16[4,8,1024]{2,0,1:T(4,128)(2,1)} %bitcast.22), calls=%async_computation | async-start | bytes 131072 | tf_op jit(solution)/shard_map/all_to_all | solution.py:40
  5.8 0.8 fusion.13
  6.6 14.1 %all_gather.10 = bf16[4,8192]{1,0:T(4,128)(2,1)} all-gather(bf16[4,2048]{1,0:T(4,128)(2,1)S(1)} %get-tuple-element.9), channel_id=1, replica_groups=mesh['dp'=8,'mp'=4] {'mp'}, dimensions={1}, use_global_device_ids=true | all-gather | bytes 81920 | tf_op jit(solution)/shard_map/all_gather | solution.py:43
  20.7 0.0 all-to-all-done
  20.7 4.3 %all-to-all-start.1 = ((bf16[4,8,1024]{2,0,1:T(4,128)(2,1)}), bf16[4,8,1024]{2,0,1:T(4,128)(2,1)S(1)}, u32[]{:S(2)}, u32[]{:S(2)}) async-start(bf16[4,8,1024]{2,0,1:T(4,128)(2,1)} %bitcast.4), calls=%async_computation.1 | async-start | bytes 131072 | tf_op jit(solution)/shard_map/all_to_all | solution.py:44
  25.0 9.7 %all-gather = bf16[8,4,2048]{2,1,0:T(4,128)(2,1)S(1)} all-gather(bf16[1,4,2048]{2,1,0:T(4,128)(2,1)S(1)} %get-tuple-element.10), channel_id=1, replica_groups=mesh['dp'=8,'mp'=4] {'dp'}, dimensions={0}, use_global_device_ids=true | all-gather | bytes 147456 | tf_op jit(solution)/shard_map/all_gather | solution.py:46
  34.7 9.2 %all-gather.1 = bf16[8,4,2048]{2,1,0:T(4,128)(2,1)S(1)} all-gather(bf16[1,4,2048]{2,1,0:T(4,128)(2,1)} %bitcast.23), channel_id=1, replica_groups=mesh['dp'=8,'mp'=4] {'dp'}, dimensions={0}, use_global_device_ids=true | all-gather | bytes 147456 | tf_op jit(solution)/shard_map/all_gather | solution.py:48
  44.0 0.0 all-to-all-done.1
  44.0 1.3 fusion.6
  45.3 0.0 copy-start
  45.3 7.8 %multiply_reduce_fusion = (f32[]{:T(128)}, f32[1024,2048]{1,0:T(8,128)}) fusion(f32[1024,2048]{1,0:T(8,128)S(1)} %fusion.6, bf16[32,1024]{1,0:T(8,128)(2,1)S(1)} %all_to_all.35, bf16[32,2048]{1,0:T(8,128)(2,1)S(1)} %reshape.19), kind=kOutput, calls=%fused_computation.6 | convolution fusion | flops 146800640 | bytes 16973828 | tf_op jit(solution)/shard_map/dot_general | solution.py:19
  53.1 0.0 copy-done
  53.1 1.3 fusion.5
  54.3 0.0 copy-start.1
  54.4 7.7 %fusion.2 = (f32[]{:T(128)}, f32[2048,1024]{0,1:T(8,128)}) fusion(f32[1024,2048]{1,0:T(8,128)S(1)} %fusion.5, bf16[32,2048]{1,0:T(8,128)(2,1)S(1)} %reshape.17, bf16[32,1024]{1,0:T(8,128)(2,1)S(1)} %all_to_all.31), kind=kOutput, calls=%fused_computation.4 | convolution fusion | flops 146800640 | bytes 16973828 | tf_op jit(solution)/shard_map/dot_general | solution.py:19
  62.0 0.0 copy-done.1
  63.3 39.4 %psum.7 = f32[]{:T(128)} all-reduce(f32[]{:T(128)S(6)} %add.21), channel_id=1, replica_groups=mesh['dp'=8,'mp'=4] {'dp','mp'}, use_global_device_ids=true, to_apply=%region_2.0 | all-reduce | flops 1 | bytes 8 | tf_op jit(solution)/shard_map/psum | solution.py:52
  103.5 29.9 %fusion = (f32[1024,2048]{1,0:T(8,128)}, f32[1024,2048]{1,0:T(8,128)}, f32[1024,2048]{1,0:T(8,128)}, f32[1024,2048]{1,0:T(8,128)}) fusion(f32[2048,1024]{0,1:T(8,128)} %get-tuple-element.12, f32[1024,2048]{1,0:T(8,128)} %copy-done.1, f32[]{:T(128)S(6)} %sqrt.3, f32[1024,2048]{1,0:T(8,128)} %copy-done, f32[1024,2048]{1,0:T(8,128)} %get-tuple-element.14), kind=kLoop, calls=%fused_computation.2 | loop fusion | flops 20971520 | bytes 67108864 | tf_op jit(solution)/shard_map/mul | solution.py:54
  (4 shorter events, 0.1 us)
Async XLA Ops:
  0.6 20.1 %all-to-all-start = ((bf16[4,8,1024]{2,0,1:T(4,128)(2,1)}), bf16[4,8,1024]{2,0,1:T(4,128)(2,1)S(1)}, u32[]{:S(2)}, u32[]{:S(2)}) async-start(bf16[4,8,1024]{2,0,1:T(4,128)(2,1)} %bitcast.22), calls=%async_computation | async-start | bytes 131072 | tf_op jit(solution)/shard_map/all_to_all | solution.py:40
  20.7 23.2 %all-to-all-start.1 = ((bf16[4,8,1024]{2,0,1:T(4,128)(2,1)}), bf16[4,8,1024]{2,0,1:T(4,128)(2,1)S(1)}, u32[]{:S(2)}, u32[]{:S(2)}) async-start(bf16[4,8,1024]{2,0,1:T(4,128)(2,1)} %bitcast.4), calls=%async_computation.1 | async-start | bytes 131072 | tf_op jit(solution)/shard_map/all_to_all | solution.py:44
  45.3 7.8 %copy-start = (f32[1024,2048]{1,0:T(8,128)}, f32[1024,2048]{1,0:T(8,128)S(1)}, u32[]{:S(2)}) copy-start(f32[1024,2048]{1,0:T(8,128)S(1)} %fusion.6) | copy-start | bytes 25165828
  54.3 7.7 %copy-start.1 = (f32[1024,2048]{1,0:T(8,128)}, f32[1024,2048]{1,0:T(8,128)S(1)}, u32[]{:S(2)}) copy-start(f32[1024,2048]{1,0:T(8,128)S(1)} %fusion.5) | copy-start | bytes 25165828
where the time goes:
time: 134 us; the launch traced here: 133 us
  blocking collectives  72.4 us (54%)
  other arithmetic  30.6 us (23%)
  matrix products  18 us (13%)
  starting transfers between devices  9.48 us (7%)
  between operations  2.7 us (2%)
    psum x1, blocking collectives, shards(): sq_norm = lax.psum(term_in + term_out, ('dp', 'mp'))  39.4 us
    mul x1, other arithmetic, shards(): direction_in = gradient_in / precond_in * rescale  29.9 us
    dot_general x2, matrix products, accumulate(): lax.dot_general(act_block, adj_piece, contract, preferred_element_type=jn...  15.4 us
    all_gather x1, blocking collectives, shards(): wide_hidden = lax.all_gather(hidden, 'mp', axis=1, tiled=True)  14.1 us
    all_gather x1, blocking collectives, shards(): lax.all_gather(adjoint, 'dp', axis=0, tiled=True)  9.71 us
    all_gather x1, blocking collectives, shards(): lax.all_gather(output_adjoint, 'dp', axis=0, tiled=True)  9.16 us
    all_to_all x1, starting transfers between devices, shards(): lax.all_to_all(layer_input, 'dp', split_axis=1, concat_axis=0, tiled=True)  5.21 us
    all_to_all x1, starting transfers between devices, shards(): lax.all_to_all(wide_hidden, 'dp', split_axis=1, concat_axis=0, tiled=True)  4.27 us
  transfers between devices with their start and end apart: 2, of which 0 were waited for; matrix products, arithmetic and copies ran while one was open for 1% of the time, Pallas kernels for 0%

commit v1 on v0

--- a/solution.py
+++ b/solution.py
@@ -49,7 +49,9 @@
     )
     gradient_in, precond_in, term_in = finish(sums_in, total_rows)
     gradient_out, precond_out, term_out = finish(sums_out, total_rows)
-    sq_norm = lax.psum(term_in + term_out, ("dp", "mp"))
+    sq_norm = term_in + term_out
+    for axis in ("mp", "dp"):
+        sq_norm = lax.psum(sq_norm, axis)
     rescale = jnp.sqrt(2.0 * D * H / sq_norm)
     direction_in = gradient_in / precond_in * rescale
     direction_out = gradient_out / precond_out * rescale

time: 134 us -> 119 us (0.89)
  blocking collectives: 72.4 us -> 57.7 us
    psum x1 -> x2, blocking collectives: 39.4 us -> 24.8 us  [shards(): sq_norm = lax.psum(sq_norm, axis)]
where the time goes in v1:
time: 119 us
  blocking collectives  57.7 us (48%)
  other arithmetic  30.6 us (26%)
  matrix products  18 us (15%)
  starting transfers between devices  9.48 us (8%)
  between operations  2.75 us (2%)
    mul x1, other arithmetic, shards(): direction_in = gradient_in / precond_in * rescale  29.9 us
    psum x2, blocking collectives, shards(): sq_norm = lax.psum(sq_norm, axis)  24.8 us
    dot_general x2, matrix products, accumulate(): lax.dot_general(act_block, adj_piece, contract, preferred_element_type=jn...  15.5 us
    all_gather x1, blocking collectives, shards(): wide_hidden = lax.all_gather(hidden, 'mp', axis=1, tiled=True)  14.1 us
    all_gather x1, blocking collectives, shards(): lax.all_gather(adjoint, 'dp', axis=0, tiled=True)  9.71 us
    all_gather x1, blocking collectives, shards(): lax.all_gather(output_adjoint, 'dp', axis=0, tiled=True)  9.16 us
    all_to_all x1, starting transfers between devices, shards(): lax.all_to_all(layer_input, 'dp', split_axis=1, concat_axis=0, tiled=True)  5.21 us
    all_to_all x1, starting transfers between devices, shards(): lax.all_to_all(wide_hidden, 'dp', split_axis=1, concat_axis=0, tiled=True)  4.27 us
  transfers between devices with their start and end apart: 2, of which 0 were waited for; matrix products, arithmetic and copies ran while one was open for 1% of the time, Pallas kernels for 0%

profile of v1, /device:TPU:0, one launch (start us, length us, event | category | flops | bytes accessed | tf_op | source)
XLA Modules:
  0.0 118.8 jit_solution(18145692517896413084)
XLA Ops:
  0.6 5.2 %all-to-all-start = ((bf16[4,8,1024]{2,0,1:T(4,128)(2,1)}), bf16[4,8,1024]{2,0,1:T(4,128)(2,1)S(1)}, u32[]{:S(2)}, u32[]{:S(2)}) async-start(bf16[4,8,1024]{2,0,1:T(4,128)(2,1)} %bitcast.22), calls=%async_computation | async-start | bytes 131072 | tf_op jit(solution)/shard_map/all_to_all | solution.py:40
  5.8 0.8 fusion.13
  6.6 14.1 %all_gather.10 = bf16[4,8192]{1,0:T(4,128)(2,1)} all-gather(bf16[4,2048]{1,0:T(4,128)(2,1)S(1)} %get-tuple-element.9), channel_id=1, replica_groups=mesh['dp'=8,'mp'=4] {'mp'}, dimensions={1}, use_global_device_ids=true | all-gather | bytes 81920 | tf_op jit(solution)/shard_map/all_gather | solution.py:43
  20.7 0.0 all-to-all-done
  20.7 4.3 %all-to-all-start.1 = ((bf16[4,8,1024]{2,0,1:T(4,128)(2,1)}), bf16[4,8,1024]{2,0,1:T(4,128)(2,1)S(1)}, u32[]{:S(2)}, u32[]{:S(2)}) async-start(bf16[4,8,1024]{2,0,1:T(4,128)(2,1)} %bitcast.4), calls=%async_computation.1 | async-start | bytes 131072 | tf_op jit(solution)/shard_map/all_to_all | solution.py:44
  25.0 9.7 %all-gather = bf16[8,4,2048]{2,1,0:T(4,128)(2,1)S(1)} all-gather(bf16[1,4,2048]{2,1,0:T(4,128)(2,1)S(1)} %get-tuple-element.10), channel_id=1, replica_groups=mesh['dp'=8,'mp'=4] {'dp'}, dimensions={0}, use_global_device_ids=true | all-gather | bytes 147456 | tf_op jit(solution)/shard_map/all_gather | solution.py:46
  34.7 9.2 %all-gather.1 = bf16[8,4,2048]{2,1,0:T(4,128)(2,1)S(1)} all-gather(bf16[1,4,2048]{2,1,0:T(4,128)(2,1)} %bitcast.23), channel_id=1, replica_groups=mesh['dp'=8,'mp'=4] {'dp'}, dimensions={0}, use_global_device_ids=true | all-gather | bytes 147456 | tf_op jit(solution)/shard_map/all_gather | solution.py:48
  44.0 0.0 all-to-all-done.1
  44.0 1.3 %fusion.6 = f32[1024,2048]{1,0:T(8,128)S(1)} fusion(bf16[32,2048]{1,0:T(8,128)(2,1)S(1)} %reshape.19, bf16[32,1024]{1,0:T(8,128)(2,1)S(1)} %all_to_all.35), kind=kOutput, calls=%fused_computation.14 | convolution fusion | flops 134512640 | bytes 8585216 | tf_op jit(solution)/shard_map/dot_general | solution.py:20
  45.3 0.0 copy-start
  45.3 7.8 %multiply_reduce_fusion = (f32[]{:T(128)}, f32[1024,2048]{1,0:T(8,128)}) fusion(f32[1024,2048]{1,0:T(8,128)S(1)} %fusion.6, bf16[32,1024]{1,0:T(8,128)(2,1)S(1)} %all_to_all.35, bf16[32,2048]{1,0:T(8,128)(2,1)S(1)} %reshape.19), kind=kOutput, calls=%fused_computation.6 | convolution fusion | flops 146800640 | bytes 16973828 | tf_op jit(solution)/shard_map/dot_general | solution.py:19
  53.1 0.0 copy-done
  53.1 1.3 %fusion.5 = f32[1024,2048]{1,0:T(8,128)S(1)} fusion(bf16[32,2048]{1,0:T(8,128)(2,1)S(1)} %reshape.17, bf16[32,1024]{1,0:T(8,128)(2,1)S(1)} %all_to_all.31), kind=kOutput, calls=%fused_computation.13 | convolution fusion | flops 134512640 | bytes 8585216 | tf_op jit(solution)/shard_map/dot_general | solution.py:20
  54.4 0.0 copy-start.1
  54.4 7.7 %fusion.2 = (f32[]{:T(128)}, f32[2048,1024]{0,1:T(8,128)}) fusion(f32[1024,2048]{1,0:T(8,128)S(1)} %fusion.5, bf16[32,2048]{1,0:T(8,128)(2,1)S(1)} %reshape.17, bf16[32,1024]{1,0:T(8,128)(2,1)S(1)} %all_to_all.31), kind=kOutput, calls=%fused_computation.4 | convolution fusion | flops 146800640 | bytes 16973828 | tf_op jit(solution)/shard_map/dot_general | solution.py:19
  62.1 0.0 copy-done.1
  63.4 12.2 %psum.14 = f32[]{:T(128)} all-reduce(f32[]{:T(128)S(6)} %add.23), channel_id=1, replica_groups=mesh['dp'=8,'mp'=4] {'mp'}, use_global_device_ids=true, to_apply=%region_2.0 | all-reduce | flops 1 | bytes 8 | tf_op jit(solution)/shard_map/psum | solution.py:54
  75.6 12.6 %psum.15 = f32[]{:T(128)} all-reduce(f32[]{:T(128)} %psum.14), channel_id=1, replica_groups=mesh['dp'=8,'mp'=4] {'dp'}, use_global_device_ids=true, to_apply=%region_3.0 | all-reduce | flops 1 | bytes 8 | tf_op jit(solution)/shard_map/psum | solution.py:54
  88.9 29.9 %fusion = (f32[1024,2048]{1,0:T(8,128)}, f32[1024,2048]{1,0:T(8,128)}, f32[1024,2048]{1,0:T(8,128)}, f32[1024,2048]{1,0:T(8,128)}) fusion(f32[2048,1024]{0,1:T(8,128)} %get-tuple-element.12, f32[1024,2048]{1,0:T(8,128)} %copy-done.1, f32[]{:T(128)S(6)} %sqrt.3, f32[1024,2048]{1,0:T(8,128)} %copy-done, f32[1024,2048]{1,0:T(8,128)} %get-tuple-element.14), kind=kLoop, calls=%fused_computation.2 | loop fusion | flops 20971520 | bytes 67108864 | tf_op jit(solution)/shard_map/mul | solution.py:56
  (4 shorter events, 0.1 us)
Async XLA Ops:
  0.6 20.1 %all-to-all-start = ((bf16[4,8,1024]{2,0,1:T(4,128)(2,1)}), bf16[4,8,1024]{2,0,1:T(4,128)(2,1)S(1)}, u32[]{:S(2)}, u32[]{:S(2)}) async-start(bf16[4,8,1024]{2,0,1:T(4,128)(2,1)} %bitcast.22), calls=%async_computation | async-start | bytes 131072 | tf_op jit(solution)/shard_map/all_to_all | solution.py:40
  20.7 23.2 %all-to-all-start.1 = ((bf16[4,8,1024]{2,0,1:T(4,128)(2,1)}), bf16[4,8,1024]{2,0,1:T(4,128)(2,1)S(1)}, u32[]{:S(2)}, u32[]{:S(2)}) async-start(bf16[4,8,1024]{2,0,1:T(4,128)(2,1)} %bitcast.4), calls=%async_computation.1 | async-start | bytes 131072 | tf_op jit(solution)/shard_map/all_to_all | solution.py:44
  45.3 7.8 %copy-start = (f32[1024,2048]{1,0:T(8,128)}, f32[1024,2048]{1,0:T(8,128)S(1)}, u32[]{:S(2)}) copy-start(f32[1024,2048]{1,0:T(8,128)S(1)} %fusion.6) | copy-start | bytes 25165828
  54.4 7.7 %copy-start.1 = (f32[1024,2048]{1,0:T(8,128)}, f32[1024,2048]{1,0:T(8,128)S(1)}, u32[]{:S(2)}) copy-start(f32[1024,2048]{1,0:T(8,128)S(1)} %fusion.5) | copy-start | bytes 25165828
